TPU v7x, 32 devices: a whole 2x2x4 slice. The times are simulated.
32 devices in a mesh: grp: 2 (over y), kv: 8 (over z, core), hd: 2 (over x), sub: 1.
Axes of the slice: x: 2, y: 2, z: 4, core: 2. Of those that a mesh axis runs over, the one named last changes fastest.
Arguments:
- queries: bfloat16 [256, 8192], P(('grp', 'kv'), 'hd'), parts along dimension 0, may hold values from -12 to 12
- prompt_of: int32 [256, 1], P('grp'), parts along dimension 0, may hold values from 0 to 1; in each aligned block of 16 rows (0 to 15, 16 to 31, ...) at most 8 rows name the same one
- prompt_len: int32 [4], P('grp'), parts along dimension 0, may hold values from 3072 to 4096
- suffix_len: int32 [256], P(('grp', 'kv')), parts along dimension 0, may hold values from 0 to 512
- page_table: int32 [256, 8], P(('grp', 'kv'), 'sub'), parts along dimension 0, may hold values from 0 to 127, as said below
- prompt_keys: bfloat16 [16384, 1024], P(('grp', 'kv', 'sub'), 'hd'), parts along dimension 0, may hold values from -14 to 14
- shared_prompt_values: bfloat16 [16384, 1024], P(('grp', 'kv', 'sub'), 'hd'), parts along dimension 0, may hold values from -6 to 6
- suffix_pool_keys: bfloat16 [2048, 64, 1024], P(('grp', 'kv', 'sub'), None, 'hd'), parts along dimension 0, may hold values from -14 to 14
- suffix_pool_values: bfloat16 [2048, 64, 1024], P(('grp', 'kv', 'sub'), None, 'hd'), parts along dimension 0, may hold values from -6 to 6
Outputs:
- attended: float32 [256, 8192], P(('grp', 'kv'), 'hd'), parts along dimension 0
There are 2 independent parts, one for each index of `grp`. A program takes and returns all parts, laid end to end along the dimension named above; each array names one. Nothing has to cross between parts.
Inputs may be any that keep to these rules, and one draw needn't show every extreme that they name: `prompt_of`: in each aligned block of 16 rows (the sequences of one index of kv), every prompt is named by exactly 8 rows. `page_table`: for each index k of kv and s of sub, the entries in rows k * 16 to (k + 1) * 16 - 1 and columns s * 8 to (s + 1) * 8 - 1 are a permutation of 0 to 127.
All inputs are finite; a program needn't handle non-finite values.
Results may differ from a plain program's by a relative error of at most 0.0011.
Values may be sent and summed in bfloat16 or wider, within the bound.
No kernel may reach another device: no remote copies, remote signals or barrier semaphores. Data moves between devices by JAX's collectives and lax.ppermute only.
A program may use at most 128 MiB of HBM per device.

v0:
```python
import math
import jax
import jax.numpy as jnp
from jax import lax
from jax.sharding import PartitionSpec as P

HEAD_SIZE = 128
NEGATIVE = -1e30


def joined(value, axis, combine):
    everything = jax.tree.map(lambda part: lax.all_gather(part, axis), value)
    leading = jax.tree.map(lambda part: part[0], everything)

    def hop(k, so_far):
        return combine(so_far, jax.tree.map(lambda part: part[k], everything))

    return lax.fori_loop(1, lax.axis_size(axis), hop, leading)


def attend_block(sent_rows, key_block, value_block, lower_bound, upper_bound, first_position):
    row_count = sent_rows.shape[0]
    key_count = key_block.shape[0]
    kv_local = key_block.shape[1] // HEAD_SIZE
    query_group_size = sent_rows.shape[1] // (HEAD_SIZE * kv_local)
    position = first_position + jnp.arange(key_count, dtype=jnp.int32)
    key_mask = (position[None, :] >= lower_bound[:, None]) & (
        position[None, :] < upper_bound[:, None]
    )
    key_mask = key_mask[:, None, :]
    score_scale = 1.0 / math.sqrt(HEAD_SIZE)
    blended_parts = []
    lse_parts = []
    for kv_head in range(kv_local):
        low_column = kv_head * query_group_size * HEAD_SIZE
        head_query = sent_rows[:, low_column : low_column + query_group_size * HEAD_SIZE].reshape(
            row_count * query_group_size, HEAD_SIZE
        )
        head_keys = key_block[:, kv_head * HEAD_SIZE : (kv_head + 1) * HEAD_SIZE]
        head_values = value_block[:, kv_head * HEAD_SIZE : (kv_head + 1) * HEAD_SIZE]
        scores = lax.dot_general(
            head_query, head_keys, (((1,), (1,)), ((), ())), preferred_element_type=jnp.float32
        )
        scores = (scores * score_scale).reshape(row_count, query_group_size, key_count)
        scores = jnp.where(key_mask, scores, NEGATIVE)
        row_max = jnp.max(scores, axis=2, keepdims=True)
        weights = jnp.where(key_mask, jnp.exp(scores - row_max), 0.0)
        totals = jnp.maximum(jnp.sum(weights, axis=2), 1.0)
        weighted = jnp.dot(
            weights.astype(jnp.bfloat16).reshape(row_count * query_group_size, key_count),
            head_values,
            preferred_element_type=jnp.float32,
        )
        weighted = weighted.reshape(row_count, query_group_size, HEAD_SIZE) / totals[:, :, None]
        blended_parts.append(weighted.reshape(row_count, query_group_size * HEAD_SIZE))
        lse_parts.append(row_max[:, :, 0] + jnp.log(totals))
    return (jnp.concatenate(blended_parts, axis=1), jnp.concatenate(lse_parts, axis=1))


def combine_halves(earlier, later):
    joint_max = jnp.maximum(earlier[0], later[0])
    left_factor = jnp.exp(earlier[0] - joint_max)
    right_factor = jnp.exp(later[0] - joint_max)
    totals = earlier[1] * left_factor + later[1] * right_factor
    blended = earlier[2] * left_factor[:, :, None] + later[2] * right_factor[:, :, None]
    return (joint_max, totals, blended)


def shards(
    queries,
    prompt_of,
    prompt_len,
    suffix_len,
    page_table,
    prompt_keys,
    shared_prompt_values,
    suffix_pool_keys,
    suffix_pool_values,
):
    kv_count = lax.axis_size("kv")
    sub_count = lax.axis_size("sub")
    kv_index = lax.axis_index("kv")
    sub_index = lax.axis_index("sub")
    seq_local = queries.shape[0]
    row_width = queries.shape[1]
    heads_local = row_width // HEAD_SIZE
    cache_local = prompt_keys.shape[0]
    kv_reach = sub_count * cache_local
    prompt_count = prompt_len.shape[0]
    prompt_starts = jnp.cumsum(prompt_len) - prompt_len
    prompt_ends = prompt_starts + prompt_len
    prompt_labels = jnp.arange(prompt_count, dtype=jnp.int32)
    range_low = jnp.arange(kv_count, dtype=jnp.int32) * kv_reach
    intersections = (prompt_starts[None, :] < range_low[:, None] + kv_reach) & (
        prompt_ends[None, :] > range_low[:, None]
    )
    later_slot = prompt_starts[None, :] > range_low[:, None]
    first_position = (kv_index * sub_count + sub_index) * cache_local
    most_rows = seq_local // prompt_count
    owned_prompt = lax.dynamic_slice_in_dim(prompt_of[:, 0], kv_index * seq_local, seq_local)
    prompt_hits = owned_prompt[:, None] == prompt_labels[None, :]
    hit_counts = prompt_hits.astype(jnp.int32)
    ranks = jnp.sum((jnp.cumsum(hit_counts, axis=0) - hit_counts) * hit_counts, axis=1)
    seq_intersection = jnp.any(intersections[:, None, :] & prompt_hits[None, :, :], axis=2)
    seq_later = jnp.any(later_slot[:, None, :] & prompt_hits[None, :, :], axis=2).astype(jnp.int32)
    slot_labels = jnp.arange(2, dtype=jnp.int32)
    rank_labels = jnp.arange(most_rows, dtype=jnp.int32)
    selector = seq_intersection[:, None, None, :] & (
        seq_later[:, None, None, :] == slot_labels[None, :, None, None]
    )
    selector = selector & (ranks[None, None, None, :] == rank_labels[None, None, :, None])
    selector = selector.reshape(kv_count * 2 * most_rows, seq_local)
    outgoing = jnp.dot(
        selector.astype(jnp.bfloat16), queries, preferred_element_type=jnp.float32
    ).astype(jnp.bfloat16)
    incoming = lax.all_to_all(
        outgoing.reshape(kv_count, 2 * most_rows, row_width),
        "kv",
        split_axis=0,
        concat_axis=0,
        tiled=True,
    )
    mine_intersection = lax.dynamic_index_in_dim(intersections, kv_index, 0, keepdims=False)
    mine_later = lax.dynamic_index_in_dim(later_slot, kv_index, 0, keepdims=False).astype(jnp.int32)
    chosen = mine_intersection[None, :] & (mine_later[None, :] == slot_labels[:, None])
    slot_low = jnp.sum(jnp.where(chosen, prompt_starts[None, :], 0), axis=1)
    slot_high = jnp.sum(jnp.where(chosen, prompt_ends[None, :], 0), axis=1)
    lower_bound = jnp.broadcast_to(
        jnp.repeat(slot_low, most_rows)[None, :], (kv_count, 2 * most_rows)
    ).reshape(-1)
    upper_bound = jnp.broadcast_to(
        jnp.repeat(slot_high, most_rows)[None, :], (kv_count, 2 * most_rows)
    ).reshape(-1)
    sent_rows = incoming.reshape(kv_count * 2 * most_rows, row_width)
    back_rows = 2 * most_rows
    prompt_out, prompt_lse = attend_block(
        sent_rows, prompt_keys, shared_prompt_values, lower_bound, upper_bound, first_position
    )
    returned_out, returned_lse = (
        lax.all_to_all(
            prompt_out.reshape(kv_count, back_rows, row_width),
            "kv",
            split_axis=0,
            concat_axis=0,
            tiled=True,
        ),
        lax.all_to_all(
            prompt_lse.reshape(kv_count, back_rows, heads_local),
            "kv",
            split_axis=0,
            concat_axis=0,
            tiled=True,
        ),
    )
    page_slots = page_table.shape[1]
    page_length = suffix_pool_keys.shape[1]
    suffix_span = page_slots * page_length
    gathered_keys = suffix_pool_keys[page_table].reshape(seq_local, suffix_span, -1)
    gathered_values = suffix_pool_values[page_table].reshape(seq_local, suffix_span, -1)
    suffix_first = sub_index * suffix_span

    def one_sequence(query_line, seq_keys, seq_values, seq_length):
        return attend_block(
            query_line[None, :],
            seq_keys,
            seq_values,
            jnp.zeros((1,), jnp.int32),
            seq_length[None],
            suffix_first,
        )

    suffix_out, suffix_lse = jax.vmap(one_sequence)(
        queries, gathered_keys, gathered_values, suffix_len
    )
    suffix_out = suffix_out[:, 0].reshape(seq_local, heads_local, HEAD_SIZE)
    suffix_lse = suffix_lse[:, 0]
    flat_lse = returned_lse.reshape(-1, heads_local)
    flat_out = returned_out.reshape(-1, heads_local, HEAD_SIZE)
    masked_lse = jnp.where(selector[:, :, None], flat_lse[:, None, :], NEGATIVE)
    joint_max = jnp.maximum(jnp.max(masked_lse, axis=0), suffix_lse)
    factors = jnp.where(selector[:, :, None], jnp.exp(masked_lse - joint_max[None]), 0.0)
    own_factor = jnp.exp(suffix_lse - joint_max)
    totals = jnp.sum(factors, axis=0) + own_factor
    blended = jnp.einsum("rsh,rhd->shd", factors, flat_out, precision=lax.Precision.HIGHEST)
    blended = blended + own_factor[:, :, None] * suffix_out
    joint_max, totals, blended = joined((joint_max, totals, blended), "sub", combine_halves)
    return (blended / totals[:, :, None]).reshape(seq_local, row_width).astype(jnp.float32)


def solution(mesh):
    placed = (
        P(("grp", "kv"), "hd"),
        P("grp", None),
        P("grp"),
        P(("grp", "kv")),
        P(("grp", "kv"), "sub"),
        P(("grp", "kv", "sub"), "hd"),
        P(("grp", "kv", "sub"), "hd"),
        P(("grp", "kv", "sub"), None, "hd"),
        P(("grp", "kv", "sub"), None, "hd"),
    )
    return jax.shard_map(
        shards, mesh=mesh, in_specs=placed, out_specs=P(("grp", "kv"), "hd"), check_vma=False
    )
```

profile of v0, /device:TPU:0, one launch (start us, length us, event | category | flops | bytes accessed | tf_op | source)
XLA Modules:
  0.0 137.8 jit_solution(13117448288514897727)
XLA Ops:
  0.0 0.8 reduce-window.8
  0.8 0.7 bitcast_subtract_fusion
  1.7 0.2 select_reduce_fusion.1
  2.4 2.3 %convolution_convert_fusion = bf16[128,4096]{1,0:T(8,128)(2,1)} fusion(pred[128,16]{1,0:T(8,128)(4,1)S(1)} %bitcast.195, bf16[16,4096]{1,0:T(8,128)(2,1)} %param.9), kind=kOutput, calls=%fused_computation.10 | convolution fusion | flops 17301504 | bytes 1181696 | tf_op jit(solution)/shard_map/dot_general | solution.py:113
  4.7 6.4 %all-to-all-start = ((bf16[8,16,4096]{2,1,0:T(8,128)(2,1)}), bf16[8,16,4096]{2,1,0:T(8,128)(2,1)S(1)}, u32[]{:S(2)}, u32[]{:S(2)}) async-start(bf16[8,16,4096]{2,1,0:T(8,128)(2,1)} %bitcast.7), calls=%async_computation | async-start | bytes 2097152 | tf_op jit(solution)/shard_map/all_to_all | solution.py:116
  11.1 0.2 select_reduce_fusion.3
  11.8 0.7 compare_select_fusion
  12.7 0.8 slice_bitcast_fusion.1
  13.5 10.0 %gather_fusion.1 = bf16[128,64,512]{2,1,0:T(8,128)(2,1)} fusion(bf16[128,64,512]{2,1,0:T(8,128)(2,1)} %param.17, s32[1024]{0:T(1024)S(1)} %pad_clamp_fusion), kind=kCustom, calls=%fused_computation.1 | custom fusion | bytes 16777728 | tf_op jit(solution)/shard_map/gather | solution.py:159
  23.5 10.0 %gather_fusion = bf16[128,64,512]{2,1,0:T(8,128)(2,1)} fusion(bf16[128,64,512]{2,1,0:T(8,128)(2,1)} %param.16, s32[1024]{0:T(1024)S(1)} %pad_clamp_fusion), kind=kCustom, calls=%fused_computation | custom fusion | bytes 16777728 | tf_op jit(solution)/shard_map/gather | solution.py:158
  33.6 0.2 compare_and_fusion
  33.8 3.9 %all-to-all-done = bf16[8,16,4096]{2,1,0:T(8,128)(2,1)S(1)} async-done(((bf16[8,16,4096]{2,1,0:T(8,128)(2,1)}), bf16[8,16,4096]{2,1,0:T(8,128)(2,1)S(1)}, u32[]{:S(2)}, u32[]{:S(2)}) %all-to-all-start) | async-done | bytes 1048608 | tf_op jit(solution)/shard_map/all_to_all | solution.py:116
  37.7 0.1 reshape.705
  37.8 0.1 reshape.707
  38.0 0.1 reshape.706
  38.1 2.6 %fusion.130 = f32[1024,1024]{1,0:T(8,128)} fusion(bf16[1024,128]{1,0:T(8,128)(2,1)S(1)} %reshape.707, bf16[1024,512]{1,0:T(8,128)(2,1)S(1)} %copy-done.6), kind=kOutput, calls=%fused_computation.99 | convolution fusion | flops 268435456 | bytes 4718592 | tf_op jit(solution)/shard_map/dot_general | solution.py:41
  40.7 2.7 %fusion.133 = f32[1024,1024]{1,0:T(8,128)} fusion(bf16[1024,128]{1,0:T(8,128)(2,1)S(1)} %reshape.706, bf16[1024,512]{1,0:T(8,128)(2,1)S(1)} %copy-done.6), kind=kOutput, calls=%fused_computation.102 | convolution fusion | flops 268435456 | bytes 4718592 | tf_op jit(solution)/shard_map/dot_general | solution.py:41
  43.5 1.2 fusion
  44.7 1.0 copy-done.2
  45.7 6.4 %fusion.4 = (f32[1024]{0:T(1024)S(1)}, f32[1024]{0:T(1024)S(1)}, f32[1024]{0:T(1024)S(1)}, f32[1024]{0:T(1024)S(1)}, f32[1024,1024]{1,0:T(8,128)S(1)}) fusion(f32[1024,1024]{1,0:T(8,128)S(1)} %get-tuple-element.51, f32[1024]{0:T(1024)S(1)} %get-tuple-element.50, pred[128,1024]{1,0:T(8,128)(4,1)S(1)} %compare_and_fusion, f32[1024,1024]{1,0:T(8,128)} %fusion.130, ...), kind=kOutput, calls=%fused_computation.15 | convolution fusion | flops 283111424 | bytes 17453056 | tf_op jit(solution)/shard_map/dot_general | solution.py:41
  52.1 5.0 %fusion.6 = (f32[1024]{0:T(1024)S(1)}, f32[1024]{0:T(1024)S(1)}, f32[1024]{0:T(1024)S(1)}) fusion(f32[1024,1024]{1,0:T(8,128)S(1)} %copy-done.2, f32[1024]{0:T(1024)S(1)} %get-tuple-element.8, pred[128,1024]{1,0:T(8,128)(4,1)S(1)} %compare_and_fusion, f32[1024]{0:T(1024)S(1)} %get-tuple-element.7, f32[1024,1024]{1,0:T(8,128)S(1)} %copy-done.3, ...), kind=kLoop, calls=%fused_computation.17 | loop fusion | flops 15725568 | bytes 12738560 | tf_op jit(solution)/shard_map/reduce_sum | solution.py:48
  57.2 3.4 %fusion.106 = f32[128,8,128]{2,1,0:T(8,128)S(1)} fusion(f32[1024,1024]{1,0:T(8,128)} %copy-done.5, f32[1024]{0:T(1024)S(1)} %get-tuple-element.6, pred[128,1024]{1,0:T(8,128)(4,1)S(1)} %compare_and_fusion, f32[128,8]{1,0:T(8,128)S(1)} %max.138, bf16[1024,512]{1,0:T(8,128)(2,1)} %param.15), kind=kOutput, calls=%fused_computation.74 | convolution fusion | flops 273809408 | bytes 5120000 | tf_op jit(solution)/shard_map/dot_general | solution.py:49
  60.8 3.2 %fusion.109 = f32[128,8,128]{2,1,0:T(8,128)S(1)} fusion(f32[1024,1024]{1,0:T(8,128)} %fusion.130, f32[1024]{0:T(1024)S(1)} %get-tuple-element.7, pred[128,1024]{1,0:T(8,128)(4,1)S(1)} %compare_and_fusion, f32[128,8]{1,0:T(8,128)S(1)} %max.136, bf16[1024,512]{1,0:T(8,128)(2,1)} %param.15), kind=kOutput, calls=%fused_computation.75 | convolution fusion | flops 273809408 | bytes 5120000 | tf_op jit(solution)/shard_map/dot_general | solution.py:49
  64.2 3.2 %fusion.112 = f32[128,8,128]{2,1,0:T(8,128)S(1)} fusion(f32[1024,1024]{1,0:T(8,128)} %fusion.133, f32[1024]{0:T(1024)S(1)} %get-tuple-element.8, pred[128,1024]{1,0:T(8,128)(4,1)S(1)} %compare_and_fusion, f32[128,8]{1,0:T(8,128)S(1)} %max.134, bf16[1024,512]{1,0:T(8,128)(2,1)} %param.15), kind=kOutput, calls=%fused_computation.76 | convolution fusion | flops 273809408 | bytes 5120000 | tf_op jit(solution)/shard_map/dot_general | solution.py:49
  67.6 3.2 %fusion.115 = f32[128,8,128]{2,1,0:T(8,128)S(1)} fusion(f32[1024,1024]{1,0:T(8,128)} %copy-done.4, f32[1024]{0:T(1024)S(1)} %get-tuple-element.50, pred[128,1024]{1,0:T(8,128)(4,1)S(1)} %compare_and_fusion, f32[128,8]{1,0:T(8,128)S(1)} %max.132, bf16[1024,512]{1,0:T(8,128)(2,1)} %param.15), kind=kOutput, calls=%fused_computation.77 | convolution fusion | flops 273809408 | bytes 5120000 | tf_op jit(solution)/shard_map/dot_general | solution.py:49
  71.2 0.1 pad_maximum_fusion.1
  71.4 0.7 reshape.747
  72.1 3.3 %all-to-all-start.2 = ((f32[8,1,512]{2,1,0:T(1,128)}), f32[8,1,512]{2,1,0:T(1,128)S(1)}, u32[]{:S(2)}, u32[]{:S(2)}) async-start(f32[8,1,512]{2,1,0:T(1,128)} %reshape.747), calls=%async_computation.2 | async-start | bytes 32768 | tf_op jit(solution)/shard_map/all_to_all | solution.py:147
  75.4 1.5 %pad_maximum_fusion = f32[8,16,4096]{2,1,0:T(8,128)} fusion(f32[8,16,1024]{2,1,0:T(8,128)S(1)} %concatenate.25, f32[8,16,1024]{2,1,0:T(8,128)S(1)} %concatenate.24, f32[8,16,1024]{2,1,0:T(8,128)S(1)} %concatenate.23, f32[8,16,1024]{2,1,0:T(8,128)S(1)} %concatenate.22), kind=kLoop, calls=%fused_computation.43 | loop fusion | flops 1572864 | bytes 4194304 | tf_op jit(solution)/shard_map/concatenate | solution.py:57
  76.9 4.1 %all-to-all-done.2 = f32[8,1,512]{2,1,0:T(1,128)S(1)} async-done(((f32[8,1,512]{2,1,0:T(1,128)}), f32[8,1,512]{2,1,0:T(1,128)S(1)}, u32[]{:S(2)}, u32[]{:S(2)}) %all-to-all-start.2) | async-done | bytes 16416 | tf_op jit(solution)/shard_map/all_to_all | solution.py:147
  81.0 3.6 %all-to-all-start.1 = ((f32[8,16,4096]{2,1,0:T(8,128)}), f32[8,16,4096]{2,1,0:T(8,128)S(1)}, u32[]{:S(2)}, u32[]{:S(2)}) async-start(f32[8,16,4096]{2,1,0:T(8,128)} %pad_maximum_fusion), calls=%async_computation.1 | async-start | bytes 4194304 | tf_op jit(solution)/shard_map/all_to_all | solution.py:140
  84.6 2.3 %fusion.191 = (f32[16,8]{1,0:T(8,128)S(1)}, f32[16,8,512]{2,1,0:T(8,128)S(1)}) fusion(bf16[16,8,128]{2,1,0:T(8,128)(2,1)S(1)} %bitcast.206, bf16[16,512,512]{2,1,0:T(8,128)(2,1)} %bitcast.187, pred[16,512]{1,0:T(8,128)(4,1)S(1)} %iota_compare_fusion), kind=kOutput, calls=%fused_computation.201 | convolution fusion | flops 16973696 | bytes 2400768 | tf_op jit(solution)/shard_map/vmap()/dot_general | solution.py:41
  86.9 2.3 %fusion.192 = (f32[16,8]{1,0:T(8,128)S(1)}, f32[16,8,512]{2,1,0:T(8,128)S(1)}) fusion(bf16[16,8,128]{2,1,0:T(8,128)(2,1)S(1)} %bitcast.208, bf16[16,512,512]{2,1,0:T(8,128)(2,1)} %bitcast.188, pred[16,512]{1,0:T(8,128)(4,1)S(1)} %iota_compare_fusion), kind=kOutput, calls=%fused_computation.202 | convolution fusion | flops 16973696 | bytes 2400768 | tf_op jit(solution)/shard_map/vmap()/dot_general | solution.py:41
  89.3 2.3 %fusion.193 = (f32[16,8]{1,0:T(8,128)S(1)}, f32[16,8,512]{2,1,0:T(8,128)S(1)}) fusion(bf16[16,8,128]{2,1,0:T(8,128)(2,1)S(1)} %bitcast.207, bf16[16,512,512]{2,1,0:T(8,128)(2,1)} %bitcast.189, pred[16,512]{1,0:T(8,128)(4,1)S(1)} %iota_compare_fusion), kind=kOutput, calls=%fused_computation.203 | convolution fusion | flops 16973696 | bytes 2400768 | tf_op jit(solution)/shard_map/vmap()/dot_general | solution.py:41
  91.6 2.3 %fusion.194 = (f32[16,8]{1,0:T(8,128)S(1)}, f32[16,8,512]{2,1,0:T(8,128)S(1)}) fusion(bf16[16,8,128]{2,1,0:T(8,128)(2,1)S(1)} %bitcast.205, bf16[16,512,512]{2,1,0:T(8,128)(2,1)} %bitcast.190, pred[16,512]{1,0:T(8,128)(4,1)S(1)} %iota_compare_fusion), kind=kOutput, calls=%fused_computation.204 | convolution fusion | flops 16973696 | bytes 2400768 | tf_op jit(solution)/shard_map/vmap()/dot_general | solution.py:41
  93.9 0.4 fusion.139
  94.3 2.0 %fusion.103 = f32[16,8,128]{2,1,0:T(8,128)S(1)} fusion(bf16[16,512,512]{2,1,0:T(8,128)(2,1)} %bitcast.183, f32[16,8,512]{2,1,0:T(8,128)S(1)} %get-tuple-element.54, f32[16,8]{1,0:T(8,128)S(1)} %get-tuple-element.53, pred[16,512]{1,0:T(8,128)(4,1)S(1)} %iota_compare_fusion, f32[16,8]{1,0:T(8,128)S(1)} %get-tuple-element.37), kind=kOutput, calls=%fused_computation.73 | convolution fusion | flops 16990208 | bytes 2434048 | tf_op jit(solution)/shard_map/vmap()/dot_general | solution.py:49
  96.4 2.0 %fusion.100 = f32[16,8,128]{2,1,0:T(8,128)S(1)} fusion(bf16[16,512,512]{2,1,0:T(8,128)(2,1)} %bitcast.184, f32[16,8,512]{2,1,0:T(8,128)S(1)} %get-tuple-element.60, f32[16,8]{1,0:T(8,128)S(1)} %get-tuple-element.59, pred[16,512]{1,0:T(8,128)(4,1)S(1)} %iota_compare_fusion, f32[16,8]{1,0:T(8,128)S(1)} %get-tuple-element.63), kind=kOutput, calls=%fused_computation.72 | convolution fusion | flops 16990208 | bytes 2434048 | tf_op jit(solution)/shard_map/vmap()/dot_general | solution.py:49
  98.5 2.0 %fusion.97 = f32[16,8,128]{2,1,0:T(8,128)S(1)} fusion(bf16[16,512,512]{2,1,0:T(8,128)(2,1)} %bitcast.185, f32[16,8,512]{2,1,0:T(8,128)S(1)} %get-tuple-element.58, f32[16,8]{1,0:T(8,128)S(1)} %get-tuple-element.57, pred[16,512]{1,0:T(8,128)(4,1)S(1)} %iota_compare_fusion, f32[16,8]{1,0:T(8,128)S(1)} %get-tuple-element.33), kind=kOutput, calls=%fused_computation.71 | convolution fusion | flops 16990208 | bytes 2434048 | tf_op jit(solution)/shard_map/vmap()/dot_general | solution.py:49
  100.5 2.0 %fusion.94 = f32[16,8,128]{2,1,0:T(8,128)S(1)} fusion(bf16[16,512,512]{2,1,0:T(8,128)(2,1)} %bitcast.186, f32[16,8,512]{2,1,0:T(8,128)S(1)} %get-tuple-element.56, f32[16,8]{1,0:T(8,128)S(1)} %get-tuple-element.55, pred[16,512]{1,0:T(8,128)(4,1)S(1)} %iota_compare_fusion, f32[16,8]{1,0:T(8,128)S(1)} %get-tuple-element.65), kind=kOutput, calls=%fused_computation.70 | convolution fusion | flops 16990208 | bytes 2434048 | tf_op jit(solution)/shard_map/vmap()/dot_general | solution.py:49
  103.0 0.5 broadcast.458
  103.5 0.7 reduce.24
  104.3 0.2 select_reduce_fusion
  104.5 0.2 fusion.120
  104.8 28.8 %all-to-all-done.1 = f32[8,16,4096]{2,1,0:T(8,128)S(1)} async-done(((f32[8,16,4096]{2,1,0:T(8,128)}), f32[8,16,4096]{2,1,0:T(8,128)S(1)}, u32[]{:S(2)}, u32[]{:S(2)}) %all-to-all-start.1) | async-done | bytes 2097184 | tf_op jit(solution)/shard_map/all_to_all | solution.py:140
  133.6 0.4 copy.73
  133.9 3.1 %fusion.55 = f32[32,2,8,128]{3,2,1,0:T(8,128)S(1)} fusion(f32[128,32,128]{2,1,0:T(8,128)S(1)} %bitcast.182, f32[16,32,128]{2,1,0:T(8,128)S(1)} %bitcast.192, f32[16,32]{0,1:T(8,128)S(1)} %get-tuple-element.20, f32[16,32]{0,1:T(8,128)S(1)} %get-tuple-element.21, f32[16,32]{0,1:T(8,128)S(1)} %fusion.167, f32[128,32]{0,1:T(8,128)S(1)} %copy.63, ...), kind=kOutput, calls=%fused_computation.57 | convolution fusion | flops 101056512 | bytes 2646016 | tf_op jit(solution)/shard_map/rsh,rhd->shd/dot_general | solution.py:184
  137.1 0.7 copy.93
  (82 shorter events, 3.4 us)
Async XLA Ops:
  0.0 1.5 %copy-start = (s32[128,1]{0,1:T(1,128)S(1)}, s32[128,1]{0,1:T(1,128)}, u32[]{:S(2)}) copy-start(s32[128,1]{0,1:T(1,128)} %param.10) | copy-start | bytes 1540
  4.7 32.9 %all-to-all-start = ((bf16[8,16,4096]{2,1,0:T(8,128)(2,1)}), bf16[8,16,4096]{2,1,0:T(8,128)(2,1)S(1)}, u32[]{:S(2)}, u32[]{:S(2)}) async-start(bf16[8,16,4096]{2,1,0:T(8,128)(2,1)} %bitcast.7), calls=%async_computation | async-start | bytes 2097152 | tf_op jit(solution)/shard_map/all_to_all | solution.py:116
  23.5 10.0 %copy-start.7 = (s32[16]{0:T(128)S(1)}, s32[16]{0:T(128)}, u32[]{:S(2)}) copy-start(s32[16]{0:T(128)} %param.12) | copy-start | bytes 196
  33.4 4.6 %copy-start.6 = (bf16[1024,512]{1,0:T(8,128)(2,1)S(1)}, bf16[1024,512]{1,0:T(8,128)(2,1)}, u32[]{:S(2)}) copy-start(bf16[1024,512]{1,0:T(8,128)(2,1)} %param.14) | copy-start | bytes 3145732
  43.5 2.2 %copy-start.2 = (f32[1024,1024]{1,0:T(8,128)S(1)}, f32[1024,1024]{1,0:T(8,128)}, u32[]{:S(2)}) copy-start(f32[1024,1024]{1,0:T(8,128)} %fusion.133) | copy-start | bytes 12582916
  44.7 7.4 %copy-start.4 = (f32[1024,1024]{1,0:T(8,128)}, f32[1024,1024]{1,0:T(8,128)S(1)}, u32[]{:S(2)}) copy-start(f32[1024,1024]{1,0:T(8,128)S(1)} %get-tuple-element.51) | copy-start | bytes 12582916
  45.7 6.4 %copy-start.3 = (f32[1024,1024]{1,0:T(8,128)S(1)}, f32[1024,1024]{1,0:T(8,128)}, u32[]{:S(2)}) copy-start(f32[1024,1024]{1,0:T(8,128)} %fusion.130) | copy-start | bytes 12582916
  52.1 5.0 %copy-start.5 = (f32[1024,1024]{1,0:T(8,128)}, f32[1024,1024]{1,0:T(8,128)S(1)}, u32[]{:S(2)}) copy-start(f32[1024,1024]{1,0:T(8,128)S(1)} %get-tuple-element.52) | copy-start | bytes 12582916
  72.1 8.9 %all-to-all-start.2 = ((f32[8,1,512]{2,1,0:T(1,128)}), f32[8,1,512]{2,1,0:T(1,128)S(1)}, u32[]{:S(2)}, u32[]{:S(2)}) async-start(f32[8,1,512]{2,1,0:T(1,128)} %reshape.747), calls=%async_computation.2 | async-start | bytes 32768 | tf_op jit(solution)/shard_map/all_to_all | solution.py:147
  81.0 52.6 %all-to-all-start.1 = ((f32[8,16,4096]{2,1,0:T(8,128)}), f32[8,16,4096]{2,1,0:T(8,128)S(1)}, u32[]{:S(2)}, u32[]{:S(2)}) async-start(f32[8,16,4096]{2,1,0:T(8,128)} %pad_maximum_fusion), calls=%async_computation.1 | async-start | bytes 4194304 | tf_op jit(solution)/shard_map/all_to_all | solution.py:140
  102.6 35.2 %copy-start.1 = (s32[128,1]{0,1:T(1,128)S(1)}, s32[128,1]{0,1:T(1,128)}, u32[]{:S(2)}) copy-start(s32[128,1]{0,1:T(1,128)} %param.10) | copy-start | bytes 1540
where the time goes:
time: 139 us; the launch traced here: 138 us
  matrix products  48.7 us (35%)
  waiting for transfers between devices  36.7 us (26%)
  local copies, waits for them, and re-layouts  27.3 us (20%)
  starting transfers between devices  13.3 us (10%)
  other arithmetic  11.3 us (8%)
    all_to_all x1, waiting for transfers between devices, shards(): lax.all_to_all(prompt_out.reshape(kv_count, back_rows, row_width), 'kv',...  28.8 us
    dot_general x8, matrix products, attend_block(): lax.dot_general(head_query, head_keys, (((1,), (1,)), ((), ())), preferre...  22.2 us
    dot_general x8, matrix products, attend_block(): jnp.dot(weights.astype(jnp.bfloat16).reshape(row_count * query_group_size...  21.1 us
    gather x1, local copies, waits for them, and re-layouts, shards(): suffix_pool_values[page_table].reshape(seq_local, suffix_span, -1)  9.96 us
    gather x1, local copies, waits for them, and re-layouts, shards(): suffix_pool_keys[page_table].reshape(seq_local, suffix_span, -1)  9.96 us
    all_to_all x1, starting transfers between devices, shards(): lax.all_to_all(outgoing.reshape(kv_count, 2 * most_rows, row_width), 'kv'...  6.37 us
    reduce_sum x2, other arithmetic, attend_block(): totals = jnp.maximum(jnp.sum(weights, axis=2), 1.0)  5.36 us
    all_to_all x1, waiting for transfers between devices, shards(): lax.all_to_all(prompt_lse.reshape(kv_count, back_rows, heads_local), 'kv'...  4.09 us
  transfers between devices with their start and end apart: 3, of which 3 were waited for; matrix products, arithmetic and copies ran while one was open for 32% of the time, Pallas kernels for 0%

commit v1 on v0

--- a/solution.py
+++ b/solution.py
@@ -3,9 +3,24 @@
 import jax.numpy as jnp
 from jax import lax
 from jax.sharding import PartitionSpec as P
+from jax.lax import axis_index, axis_size, ppermute
 
 HEAD_SIZE = 128
 NEGATIVE = -1e30
+
+
+def number_the_sections(row_data, at_axis, xx):
+    current_block, k_now = (row_data.shape[:at_axis], row_data.shape[at_axis + 1 :])
+    view_out = row_data.reshape(*current_block, xx, -1, *k_now)
+    spare = jnp.moveaxis(view_out, at_axis, 0)
+    return spare
+
+
+def treat_shards_on(array_here, dim_i):
+    piece_next = list(array_here.shape[1:])
+    piece_next[dim_i] *= array_here.shape[0]
+    known = jnp.moveaxis(array_here, 0, dim_i).reshape(piece_next)
+    return known
 
 
 def joined(value, axis, combine):
@@ -136,6 +151,24 @@
     prompt_out, prompt_lse = attend_block(
         sent_rows, prompt_keys, shared_prompt_values, lower_bound, upper_bound, first_position
     )
+
+    def _choose_words(payload, named_axis, panel, local_array):
+        side_arr = axis_size(named_axis)
+        mixed_arr = axis_index(named_axis)
+        local_next, b_now = (side_arr, mixed_arr)
+        all_values = number_the_sections(payload, panel, local_next)
+        so_far_all = [all_values[b_now]]
+        it = 1
+        while it < local_next:
+            arr_now = all_values[b_now ^ it]
+            top = ppermute(arr_now, named_axis, [(p, p ^ it) for p in range(local_next)])
+            so_far_all.append(top)
+            it += 1
+        t1 = jnp.stack(so_far_all)
+        all_values = t1[b_now ^ jnp.arange(local_next)]
+        heard = treat_shards_on(all_values, local_array)
+        return heard
+
     returned_out, returned_lse = (
         lax.all_to_all(
             prompt_out.reshape(kv_count, back_rows, row_width),
@@ -144,12 +177,8 @@
             concat_axis=0,
             tiled=True,
         ),
-        lax.all_to_all(
-            prompt_lse.reshape(kv_count, back_rows, heads_local),
-            "kv",
-            split_axis=0,
-            concat_axis=0,
-            tiled=True,
+        _choose_words(
+            prompt_lse.reshape(kv_count, back_rows, heads_local), "kv", panel=0, local_array=0
         ),
     )
     page_slots = page_table.shape[1]

time: 139 us -> 145 us (1.043)
  starting transfers between devices: 13.3 us -> 22.4 us
  waiting for transfers between devices: 36.7 us -> 31.9 us
    ppermute x0 -> x7, waiting for transfers between devices: none -> 31.9 us  [_choose_words(): ppermute(arr_now, named_axis, [(p, p ^ it) for p in range(local_next)])]
    all_to_all x1, waiting for transfers between devices: 28.8 us -> 0.01 us  [shards(): lax.all_to_all(prompt_out.reshape(kv_count, back_rows, row_width), 'kv',...]
    ppermute x0 -> x7, starting transfers between devices: none -> 10.8 us  [_choose_words(): ppermute(arr_now, named_axis, [(p, p ^ it) for p in range(local_next)])]
    all_to_all x1 -> x0, waiting for transfers between devices: 4.09 us -> none  [shards(): lax.all_to_all(prompt_lse.reshape(kv_count, back_rows, heads_local), 'kv'...]
    all_to_all x1, waiting for transfers between devices: 3.86 us -> 0.01 us  [shards(): lax.all_to_all(outgoing.reshape(kv_count, 2 * most_rows, row_width), 'kv'...]
    all_to_all x1 -> x0, starting transfers between devices: 3.34 us -> none  [shards(): lax.all_to_all(prompt_lse.reshape(kv_count, back_rows, heads_local), 'kv'...]
    all_to_all x1, starting transfers between devices: 3.6 us -> 5.24 us  [shards(): lax.all_to_all(prompt_out.reshape(kv_count, back_rows, row_width), 'kv',...]
    unnamed x25 -> x69, local copies, waits for them, and re-layouts: 3.06 us -> 2.98 us
  transfers between devices with their start and end apart: 3 -> 9, of which waited for: 3 -> 2; matrix products, arithmetic and copies ran while one was open for 32% -> 31% of each run, Pallas kernels for 0% -> 0%
where the time goes in v1:
time: 145 us; the launch traced here: 144 us
  matrix products  49.8 us (34%)
  waiting for transfers between devices  31.9 us (22%)
  local copies, waits for them, and re-layouts  27.2 us (19%)
  starting transfers between devices  22.4 us (15%)
  other arithmetic  11.9 us (8%)
    ppermute x7, waiting for transfers between devices, _choose_words(): ppermute(arr_now, named_axis, [(p, p ^ it) for p in range(local_next)])  31.9 us
    dot_general x8, matrix products, attend_block(): lax.dot_general(head_query, head_keys, (((1,), (1,)), ((), ())), preferre...  22.9 us
    dot_general x8, matrix products, attend_block(): jnp.dot(weights.astype(jnp.bfloat16).reshape(row_count * query_group_size...  21.5 us
    ppermute x7, starting transfers between devices, _choose_words(): ppermute(arr_now, named_axis, [(p, p ^ it) for p in range(local_next)])  10.8 us
    gather x1, local copies, waits for them, and re-layouts, shards(): suffix_pool_values[page_table].reshape(seq_local, suffix_span, -1)  9.96 us
    gather x1, local copies, waits for them, and re-layouts, shards(): suffix_pool_keys[page_table].reshape(seq_local, suffix_span, -1)  9.96 us
    all_to_all x1, starting transfers between devices, shards(): lax.all_to_all(outgoing.reshape(kv_count, 2 * most_rows, row_width), 'kv'...  6.36 us
    reduce_sum x2, other arithmetic, attend_block(): totals = jnp.maximum(jnp.sum(weights, axis=2), 1.0)  6.07 us
  transfers between devices with their start and end apart: 9, of which 2 were waited for; matrix products, arithmetic and copies ran while one was open for 31% of the time, Pallas kernels for 0%

profile of v1, /device:TPU:0, one launch (start us, length us, event | category | flops | bytes accessed | tf_op | source)
XLA Modules:
  0.0 144.1 jit_solution(11416951424150058848)
XLA Ops:
  0.0 0.8 reduce-window.8
  0.8 0.7 bitcast_subtract_fusion
  1.7 0.2 select_reduce_fusion.1
  2.4 0.6 copy-done.11
  3.0 2.3 %convolution_convert_fusion = bf16[128,4096]{1,0:T(8,128)(2,1)} fusion(pred[128,16]{1,0:T(8,128)(4,1)S(1)} %bitcast.226, bf16[16,4096]{1,0:T(8,128)(2,1)} %param.9), kind=kOutput, calls=%fused_computation.11 | convolution fusion | flops 17301504 | bytes 1181696 | tf_op jit(solution)/shard_map/dot_general | solution.py:128
  5.3 6.4 %all-to-all-start = ((bf16[8,16,4096]{2,1,0:T(8,128)(2,1)}), bf16[8,16,4096]{2,1,0:T(8,128)(2,1)S(1)}, u32[]{:S(2)}, u32[]{:S(2)}) async-start(bf16[8,16,4096]{2,1,0:T(8,128)(2,1)} %bitcast.7), calls=%async_computation | async-start | bytes 2097152 | tf_op jit(solution)/shard_map/all_to_all | solution.py:131
  11.7 0.1 select_reduce_fusion.3
  12.3 0.7 compare_select_fusion
  13.2 0.8 slice_bitcast_fusion.1
  14.0 10.0 %gather_fusion.2 = bf16[128,64,512]{2,1,0:T(8,128)(2,1)} fusion(bf16[128,64,512]{2,1,0:T(8,128)(2,1)} %param.17, s32[1024]{0:T(1024)S(1)} %pad_clamp_fusion), kind=kCustom, calls=%fused_computation.2 | custom fusion | bytes 16777728 | tf_op jit(solution)/shard_map/gather | solution.py:188
  24.0 10.0 %gather_fusion.1 = bf16[128,64,512]{2,1,0:T(8,128)(2,1)} fusion(bf16[128,64,512]{2,1,0:T(8,128)(2,1)} %param.16, s32[1024]{0:T(1024)S(1)} %pad_clamp_fusion), kind=kCustom, calls=%fused_computation.1 | custom fusion | bytes 16777728 | tf_op jit(solution)/shard_map/gather | solution.py:187
  34.1 2.3 %fusion.194 = (f32[16,8]{1,0:T(8,128)S(1)}, f32[16,8,512]{2,1,0:T(8,128)S(1)}) fusion(bf16[16,8,128]{2,1,0:T(8,128)(2,1)S(1)} %bitcast.239, bf16[16,512,512]{2,1,0:T(8,128)(2,1)} %bitcast.218, pred[16,512]{1,0:T(8,128)(4,1)S(1)} %iota_compare_fusion), kind=kOutput, calls=%fused_computation.222 | convolution fusion | flops 16973696 | bytes 2400768 | tf_op jit(solution)/shard_map/vmap()/dot_general | solution.py:56
  36.4 2.3 %fusion.195 = (f32[16,8]{1,0:T(8,128)S(1)}, f32[16,8,512]{2,1,0:T(8,128)S(1)}) fusion(bf16[16,8,128]{2,1,0:T(8,128)(2,1)S(1)} %bitcast.240, bf16[16,512,512]{2,1,0:T(8,128)(2,1)} %bitcast.219, pred[16,512]{1,0:T(8,128)(4,1)S(1)} %iota_compare_fusion), kind=kOutput, calls=%fused_computation.223 | convolution fusion | flops 16973696 | bytes 2400768 | tf_op jit(solution)/shard_map/vmap()/dot_general | solution.py:56
  38.7 2.3 %fusion.196 = (f32[16,8]{1,0:T(8,128)S(1)}, f32[16,8,512]{2,1,0:T(8,128)S(1)}) fusion(bf16[16,8,128]{2,1,0:T(8,128)(2,1)S(1)} %bitcast.238, bf16[16,512,512]{2,1,0:T(8,128)(2,1)} %bitcast.220, pred[16,512]{1,0:T(8,128)(4,1)S(1)} %iota_compare_fusion), kind=kOutput, calls=%fused_computation.224 | convolution fusion | flops 16973696 | bytes 2400768 | tf_op jit(solution)/shard_map/vmap()/dot_general | solution.py:56
  41.0 2.4 %fusion.197 = (f32[16,8]{1,0:T(8,128)S(1)}, f32[16,8,512]{2,1,0:T(8,128)S(1)}) fusion(bf16[16,8,128]{2,1,0:T(8,128)(2,1)S(1)} %bitcast.237, bf16[16,512,512]{2,1,0:T(8,128)(2,1)} %bitcast.221, pred[16,512]{1,0:T(8,128)(4,1)S(1)} %iota_compare_fusion), kind=kOutput, calls=%fused_computation.225 | convolution fusion | flops 16973696 | bytes 2400768 | tf_op jit(solution)/shard_map/vmap()/dot_general | solution.py:56
  43.5 0.9 fusion.139
  44.4 0.6 log_add_fusion
  45.0 0.2 compare_and_fusion
  45.2 2.7 %fusion.103 = f32[16,8,128]{2,1,0:T(8,128)} fusion(bf16[16,512,512]{2,1,0:T(8,128)(2,1)} %bitcast.214, f32[16,8,512]{2,1,0:T(8,128)S(1)} %get-tuple-element.62, f32[16,8]{1,0:T(8,128)S(1)} %get-tuple-element.61, pred[16,512]{1,0:T(8,128)(4,1)S(1)} %iota_compare_fusion, f32[16,8]{1,0:T(8,128)S(1)} %get-tuple-element.45), kind=kOutput, calls=%fused_computation.74 | convolution fusion | flops 16990208 | bytes 2434048 | tf_op jit(solution)/shard_map/vmap()/dot_general | solution.py:64
  48.3 2.7 %fusion.130 = f32[1024,1024]{1,0:T(8,128)} fusion(bf16[1024,128]{1,0:T(8,128)(2,1)S(1)} %reshape.806, bf16[1024,512]{1,0:T(8,128)(2,1)S(1)} %copy-done.6), kind=kOutput, calls=%fused_computation.100 | convolution fusion | flops 268435456 | bytes 4718592 | tf_op jit(solution)/shard_map/dot_general | solution.py:56
  51.0 2.6 %fusion.133 = f32[1024,1024]{1,0:T(8,128)} fusion(bf16[1024,128]{1,0:T(8,128)(2,1)S(1)} %reshape.805, bf16[1024,512]{1,0:T(8,128)(2,1)S(1)} %copy-done.6), kind=kOutput, calls=%fused_computation.103 | convolution fusion | flops 268435456 | bytes 4718592 | tf_op jit(solution)/shard_map/dot_general | solution.py:56
  53.8 1.2 fusion
  55.0 1.0 copy-done.2
  56.0 7.0 %fusion.4 = (f32[1024]{0:T(1024)}, f32[1024]{0:T(1024)S(1)}, f32[1024]{0:T(1024)S(1)}, f32[1024]{0:T(1024)S(1)}, f32[1024,1024]{1,0:T(8,128)S(1)}) fusion(f32[1024,1024]{1,0:T(8,128)S(1)} %get-tuple-element.59, f32[1024]{0:T(1024)S(1)} %get-tuple-element.58, pred[128,1024]{1,0:T(8,128)(4,1)S(1)} %compare_and_fusion, f32[1024,1024]{1,0:T(8,128)} %fusion.130, ...), kind=kOutput, calls=%fused_computation.16 | convolution fusion | flops 283111424 | bytes 17453056 | tf_op jit(solution)/shard_map/dot_general | solution.py:56
  62.9 5.2 %fusion.6 = (f32[1024]{0:T(1024)S(1)}, f32[1024]{0:T(1024)S(1)}, f32[1024]{0:T(1024)S(1)}) fusion(f32[1024,1024]{1,0:T(8,128)S(1)} %copy-done.2, f32[1024]{0:T(1024)S(1)} %get-tuple-element.8, pred[128,1024]{1,0:T(8,128)(4,1)S(1)} %compare_and_fusion, f32[1024]{0:T(1024)S(1)} %get-tuple-element.7, f32[1024,1024]{1,0:T(8,128)S(1)} %copy-done.3, ...), kind=kLoop, calls=%fused_computation.18 | loop fusion | flops 15725568 | bytes 12738560 | tf_op jit(solution)/shard_map/reduce_sum | solution.py:63
  68.2 3.2 %fusion.106 = f32[128,8,128]{2,1,0:T(8,128)S(1)} fusion(f32[1024,1024]{1,0:T(8,128)} %copy-done.5, f32[1024]{0:T(1024)S(1)} %get-tuple-element.6, pred[128,1024]{1,0:T(8,128)(4,1)S(1)} %compare_and_fusion, f32[128,8]{1,0:T(8,128)S(1)} %max.162, bf16[1024,512]{1,0:T(8,128)(2,1)S(1)} %copy-done.27), kind=kOutput, calls=%fused_computation.75 | convolution fusion | flops 273809408 | bytes 5181440 | tf_op jit(solution)/shard_map/dot_general | solution.py:64
  71.6 3.2 %fusion.109 = f32[128,8,128]{2,1,0:T(8,128)S(1)} fusion(f32[1024,1024]{1,0:T(8,128)} %fusion.130, f32[1024]{0:T(1024)S(1)} %get-tuple-element.7, pred[128,1024]{1,0:T(8,128)(4,1)S(1)} %compare_and_fusion, f32[128,8]{1,0:T(8,128)S(1)} %max.160, bf16[1024,512]{1,0:T(8,128)(2,1)S(1)} %copy-done.27), kind=kOutput, calls=%fused_computation.76 | convolution fusion | flops 273809408 | bytes 5181440 | tf_op jit(solution)/shard_map/dot_general | solution.py:64
  75.0 3.2 %fusion.112 = f32[128,8,128]{2,1,0:T(8,128)S(1)} fusion(f32[1024,1024]{1,0:T(8,128)} %fusion.133, f32[1024]{0:T(1024)S(1)} %get-tuple-element.8, pred[128,1024]{1,0:T(8,128)(4,1)S(1)} %compare_and_fusion, f32[128,8]{1,0:T(8,128)S(1)} %max.158, bf16[1024,512]{1,0:T(8,128)(2,1)} %param.15), kind=kOutput, calls=%fused_computation.77 | convolution fusion | flops 273809408 | bytes 5120000 | tf_op jit(solution)/shard_map/dot_general | solution.py:64
  78.4 3.2 %fusion.115 = f32[128,8,128]{2,1,0:T(8,128)S(1)} fusion(f32[1024,1024]{1,0:T(8,128)} %copy-done.4, f32[1024]{0:T(1024)S(1)} %get-tuple-element.58, pred[128,1024]{1,0:T(8,128)(4,1)S(1)} %compare_and_fusion, f32[128,8]{1,0:T(8,128)S(1)} %max.156, bf16[1024,512]{1,0:T(8,128)(2,1)} %param.15), kind=kOutput, calls=%fused_computation.78 | convolution fusion | flops 273809408 | bytes 5120000 | tf_op jit(solution)/shard_map/dot_general | solution.py:64
  81.8 1.5 %pad_maximum_fusion = f32[8,16,4096]{2,1,0:T(8,128)} fusion(f32[8,16,1024]{2,1,0:T(8,128)S(1)} %concatenate.25, f32[8,16,1024]{2,1,0:T(8,128)S(1)} %concatenate.24, f32[8,16,1024]{2,1,0:T(8,128)S(1)} %concatenate.23, f32[8,16,1024]{2,1,0:T(8,128)S(1)} %concatenate.22), kind=kLoop, calls=%fused_computation.44 | loop fusion | flops 1572864 | bytes 4194304 | tf_op jit(solution)/shard_map/concatenate | solution.py:72
  83.3 5.2 %all-to-all-start.1 = ((f32[8,16,4096]{2,1,0:T(8,128)}), f32[8,16,4096]{2,1,0:T(8,128)S(1)}, u32[]{:S(2)}, u32[]{:S(2)}) async-start(f32[8,16,4096]{2,1,0:T(8,128)} %pad_maximum_fusion), calls=%async_computation.1 | async-start | bytes 4194304 | tf_op jit(solution)/shard_map/all_to_all | solution.py:173
  88.6 2.0 %fusion.100 = f32[16,8,128]{2,1,0:T(8,128)S(1)} fusion(bf16[16,512,512]{2,1,0:T(8,128)(2,1)} %bitcast.215, f32[16,8,512]{2,1,0:T(8,128)S(1)} %copy-done.10, f32[16,8]{1,0:T(8,128)S(1)} %copy-done.21, pred[16,512]{1,0:T(8,128)(4,1)S(1)} %iota_compare_fusion, f32[16,8]{1,0:T(8,128)S(1)} %copy-done.24), kind=kOutput, calls=%fused_computation.73 | convolution fusion | flops 16990208 | bytes 2434048 | tf_op jit(solution)/shard_map/vmap()/dot_general | solution.py:64
  90.8 2.0 %fusion.97 = f32[16,8,128]{2,1,0:T(8,128)S(1)} fusion(bf16[16,512,512]{2,1,0:T(8,128)(2,1)} %bitcast.216, f32[16,8,512]{2,1,0:T(8,128)S(1)} %copy-done.8, f32[16,8]{1,0:T(8,128)S(1)} %copy-done.17, pred[16,512]{1,0:T(8,128)(4,1)S(1)} %iota_compare_fusion, f32[16,8]{1,0:T(8,128)S(1)} %get-tuple-element.41), kind=kOutput, calls=%fused_computation.72 | convolution fusion | flops 16990208 | bytes 2434048 | tf_op jit(solution)/shard_map/vmap()/dot_general | solution.py:64
  92.9 2.0 %fusion.94 = f32[16,8,128]{2,1,0:T(8,128)S(1)} fusion(bf16[16,512,512]{2,1,0:T(8,128)(2,1)} %bitcast.217, f32[16,8,512]{2,1,0:T(8,128)S(1)} %get-tuple-element.64, f32[16,8]{1,0:T(8,128)S(1)} %copy-done.15, pred[16,512]{1,0:T(8,128)(4,1)S(1)} %iota_compare_fusion, f32[16,8]{1,0:T(8,128)S(1)} %get-tuple-element.73), kind=kOutput, calls=%fused_computation.71 | convolution fusion | flops 16990208 | bytes 2434048 | tf_op jit(solution)/shard_map/vmap()/dot_general | solution.py:64
  95.4 0.1 pad_maximum_fusion.1
  95.5 0.6 collective-permute-start
  96.6 1.6 %collective-permute-start.1 = (f32[1,16,32]{2,1,0:T(8,128)S(1)}, f32[1,16,32]{2,1,0:T(8,128)S(1)}, u32[]{:S(2)}, u32[]{:S(2)}) collective-permute-start(f32[1,16,32]{2,1,0:T(8,128)S(1)} %get-tuple-element.35), channel_id=1, source_target_pairs={{0,4},{2,6},{4,0},{6,2},{8,12},{10,14},{12,8},{14,10},{1,5},{3,7},... | collective-permute-start | bytes 6152 | tf_op jit(solution)/shard_map/ppermute | solution.py:164
  98.2 2.6 %collective-permute-start.3 = (f32[1,16,32]{2,1,0:T(8,128)S(1)}, f32[1,16,32]{2,1,0:T(8,128)S(1)}, u32[]{:S(2)}, u32[]{:S(2)}) collective-permute-start(f32[1,16,32]{2,1,0:T(8,128)S(1)} %get-tuple-element.33), channel_id=1, source_target_pairs={{0,8},{2,10},{4,12},{6,14},{8,0},{10,2},{12,4},{14,6},{1,9},{3,11}... | collective-permute-start | bytes 6152 | tf_op jit(solution)/shard_map/ppermute | solution.py:164
  101.0 3.4 %collective-permute-start.5 = (f32[1,16,32]{2,1,0:T(8,128)S(1)}, f32[1,16,32]{2,1,0:T(8,128)S(1)}, u32[]{:S(2)}, u32[]{:S(2)}) collective-permute-start(f32[1,16,32]{2,1,0:T(8,128)S(1)} %get-tuple-element.31), channel_id=1, source_target_pairs={{0,12},{2,14},{4,8},{6,10},{8,4},{10,6},{12,0},{14,2},{1,13},{3,15... | collective-permute-start | bytes 6152 | tf_op jit(solution)/shard_map/ppermute | solution.py:164
  104.4 19.4 %collective-permute-done.1 = f32[1,16,32]{2,1,0:T(8,128)S(1)} collective-permute-done((f32[1,16,32]{2,1,0:T(8,128)S(1)}, f32[1,16,32]{2,1,0:T(8,128)S(1)}, u32[]{:S(2)}, u32[]{:S(2)}) %collective-permute-start.1) | collective-permute-done | bytes 2080 | tf_op jit(solution)/shard_map/ppermute | solution.py:164
  123.8 2.4 %collective-permute-start.6 = (f32[1,16,32]{2,1,0:T(8,128)S(1)}, f32[1,16,32]{2,1,0:T(8,128)S(1)}, u32[]{:S(2)}, u32[]{:S(2)}) collective-permute-start(f32[1,16,32]{2,1,0:T(8,128)S(1)} %get-tuple-element.30), channel_id=1, source_target_pairs={{0,14},{2,12},{4,10},{6,8},{8,6},{10,4},{12,2},{14,0},{1,15},{3,13... | collective-permute-start | bytes 6152 | tf_op jit(solution)/shard_map/ppermute | solution.py:164
  126.2 12.5 %collective-permute-done.3 = f32[1,16,32]{2,1,0:T(8,128)S(1)} collective-permute-done((f32[1,16,32]{2,1,0:T(8,128)S(1)}, f32[1,16,32]{2,1,0:T(8,128)S(1)}, u32[]{:S(2)}, u32[]{:S(2)}) %collective-permute-start.3) | collective-permute-done | bytes 2080 | tf_op jit(solution)/shard_map/ppermute | solution.py:164
  138.8 0.6 gather_fusion
  139.4 0.2 select_reduce_fusion
  139.6 0.2 fusion.120
  139.9 0.4 copy.73
  140.3 3.1 %fusion.55 = f32[32,2,8,128]{3,2,1,0:T(8,128)S(1)} fusion(f32[128,32,128]{2,1,0:T(8,128)S(1)} %bitcast.213, f32[16,32,128]{2,1,0:T(8,128)S(1)} %bitcast.223, f32[16,32]{0,1:T(8,128)S(1)} %get-tuple-element.20, f32[16,32]{0,1:T(8,128)S(1)} %get-tuple-element.21, f32[16,32]{0,1:T(8,128)S(1)} %fusion.167, f32[128,32]{0,1:T(8,128)S(1)} %copy.63, ...), kind=kOutput, calls=%fused_computation.58 | convolution fusion | flops 101056512 | bytes 2646016 | tf_op jit(solution)/shard_map/rsh,rhd->shd/dot_general | solution.py:213
  143.4 0.7 copy.93
  (141 shorter events, 3.9 us)
Async XLA Ops:
  0.0 1.5 %copy-start = (s32[128,1]{0,1:T(1,128)S(1)}, s32[128,1]{0,1:T(1,128)}, u32[]{:S(2)}) copy-start(s32[128,1]{0,1:T(1,128)} %param.10) | copy-start | bytes 1540
  2.4 0.6 copy-start.11
  5.3 42.6 %all-to-all-start = ((bf16[8,16,4096]{2,1,0:T(8,128)(2,1)}), bf16[8,16,4096]{2,1,0:T(8,128)(2,1)S(1)}, u32[]{:S(2)}, u32[]{:S(2)}) async-start(bf16[8,16,4096]{2,1,0:T(8,128)(2,1)} %bitcast.7), calls=%async_computation | async-start | bytes 2097152 | tf_op jit(solution)/shard_map/all_to_all | solution.py:131
  24.0 10.0 %copy-start.26 = (s32[16]{0:T(128)S(1)}, s32[16]{0:T(128)}, u32[]{:S(2)}) copy-start(s32[16]{0:T(128)} %param.12) | copy-start | bytes 196
  38.7 5.7 %copy-start.14 = (f32[16,8]{1,0:T(8,128)}, f32[16,8]{1,0:T(8,128)S(1)}, u32[]{:S(2)}) copy-start(f32[16,8]{1,0:T(8,128)S(1)} %get-tuple-element.63) | copy-start | bytes 1540
  41.0 3.4 %copy-start.16 = (f32[16,8]{1,0:T(8,128)}, f32[16,8]{1,0:T(8,128)S(1)}, u32[]{:S(2)}) copy-start(f32[16,8]{1,0:T(8,128)S(1)} %get-tuple-element.65) | copy-start | bytes 1540
  41.0 6.8 %copy-start.7 = (f32[16,8,512]{2,1,0:T(8,128)}, f32[16,8,512]{2,1,0:T(8,128)S(1)}, u32[]{:S(2)}) copy-start(f32[16,8,512]{2,1,0:T(8,128)S(1)} %get-tuple-element.66) | copy-start | bytes 786436
  43.5 0.9 copy-start.20
  43.5 4.4 %copy-start.9 = (f32[16,8,512]{2,1,0:T(8,128)}, f32[16,8,512]{2,1,0:T(8,128)S(1)}, u32[]{:S(2)}) copy-start(f32[16,8,512]{2,1,0:T(8,128)S(1)} %get-tuple-element.68) | copy-start | bytes 786436
  43.5 4.9 %copy-start.6 = (bf16[1024,512]{1,0:T(8,128)(2,1)S(1)}, bf16[1024,512]{1,0:T(8,128)(2,1)}, u32[]{:S(2)}) copy-start(bf16[1024,512]{1,0:T(8,128)(2,1)} %param.14) | copy-start | bytes 3145732
  53.7 2.2 %copy-start.2 = (f32[1024,1024]{1,0:T(8,128)S(1)}, f32[1024,1024]{1,0:T(8,128)}, u32[]{:S(2)}) copy-start(f32[1024,1024]{1,0:T(8,128)} %fusion.133) | copy-start | bytes 12582916
  55.0 7.9 %copy-start.4 = (f32[1024,1024]{1,0:T(8,128)}, f32[1024,1024]{1,0:T(8,128)S(1)}, u32[]{:S(2)}) copy-start(f32[1024,1024]{1,0:T(8,128)S(1)} %get-tuple-element.59) | copy-start | bytes 12582916
  56.0 7.0 %copy-start.3 = (f32[1024,1024]{1,0:T(8,128)S(1)}, f32[1024,1024]{1,0:T(8,128)}, u32[]{:S(2)}) copy-start(f32[1024,1024]{1,0:T(8,128)} %fusion.130) | copy-start | bytes 12582916
  62.9 5.2 %copy-start.5 = (f32[1024,1024]{1,0:T(8,128)}, f32[1024,1024]{1,0:T(8,128)S(1)}, u32[]{:S(2)}) copy-start(f32[1024,1024]{1,0:T(8,128)S(1)} %get-tuple-element.60) | copy-start | bytes 12582916
  62.9 5.3 %copy-start.27 = (bf16[1024,512]{1,0:T(8,128)(2,1)S(1)}, bf16[1024,512]{1,0:T(8,128)(2,1)}, u32[]{:S(2)}) copy-start(bf16[1024,512]{1,0:T(8,128)(2,1)} %param.15) | copy-start | bytes 3145732
  75.0 3.3 %copy-start.25 = (f32[1024]{0:T(1024)S(1)}, f32[1024]{0:T(1024)}, u32[]{:S(2)}) copy-start(f32[1024]{0:T(1024)} %get-tuple-element.5) | copy-start | bytes 12292
  81.7 6.8 %copy-start.10 = (f32[16,8,512]{2,1,0:T(8,128)S(1)}, f32[16,8,512]{2,1,0:T(8,128)}, u32[]{:S(2)}) copy-start(f32[16,8,512]{2,1,0:T(8,128)} %copy-done.9) | copy-start | bytes 786436
  81.7 6.8 %copy-start.21 = (f32[16,8]{1,0:T(8,128)S(1)}, f32[16,8]{1,0:T(8,128)}, u32[]{:S(2)}) copy-start(f32[16,8]{1,0:T(8,128)} %copy-done.20) | copy-start | bytes 1540
  81.7 6.8 %copy-start.24 = (f32[16,8]{1,0:T(8,128)S(1)}, f32[16,8]{1,0:T(8,128)}, u32[]{:S(2)}) copy-start(f32[16,8]{1,0:T(8,128)} %get-tuple-element.71) | copy-start | bytes 1540
  83.3 7.4 %copy-start.13 = (f32[16,8,128]{2,1,0:T(8,128)S(1)}, f32[16,8,128]{2,1,0:T(8,128)}, u32[]{:S(2)}) copy-start(f32[16,8,128]{2,1,0:T(8,128)} %fusion.103) | copy-start | bytes 196612
  83.3 7.4 %copy-start.15 = (f32[16,8]{1,0:T(8,128)S(1)}, f32[16,8]{1,0:T(8,128)}, u32[]{:S(2)}) copy-start(f32[16,8]{1,0:T(8,128)} %copy-done.14) | copy-start | bytes 1540
  83.3 7.5 %copy-start.17 = (f32[16,8]{1,0:T(8,128)S(1)}, f32[16,8]{1,0:T(8,128)}, u32[]{:S(2)}) copy-start(f32[16,8]{1,0:T(8,128)} %copy-done.16) | copy-start | bytes 1540
  83.3 7.5 %copy-start.18 = (f32[16,8]{1,0:T(8,128)S(1)}, f32[16,8]{1,0:T(8,128)}, u32[]{:S(2)}) copy-start(f32[16,8]{1,0:T(8,128)} %get-tuple-element.12) | copy-start | bytes 1540
  83.3 7.5 %copy-start.19 = (f32[16,8]{1,0:T(8,128)S(1)}, f32[16,8]{1,0:T(8,128)}, u32[]{:S(2)}) copy-start(f32[16,8]{1,0:T(8,128)} %get-tuple-element.13) | copy-start | bytes 1540
  83.3 7.5 %copy-start.8 = (f32[16,8,512]{2,1,0:T(8,128)S(1)}, f32[16,8,512]{2,1,0:T(8,128)}, u32[]{:S(2)}) copy-start(f32[16,8,512]{2,1,0:T(8,128)} %copy-done.7) | copy-start | bytes 786436
  83.3 56.5 %all-to-all-start.1 = ((f32[8,16,4096]{2,1,0:T(8,128)}), f32[8,16,4096]{2,1,0:T(8,128)S(1)}, u32[]{:S(2)}, u32[]{:S(2)}) async-start(f32[8,16,4096]{2,1,0:T(8,128)} %pad_maximum_fusion), calls=%async_computation.1 | async-start | bytes 4194304 | tf_op jit(solution)/shard_map/all_to_all | solution.py:173
  90.6 5.5 %copy-start.12 = (pred[8,2,8,16]{3,2,1,0:T(8,128)(4,1)S(1)}, pred[8,2,8,16]{3,2,1,0:T(8,128)(4,1)}, u32[]{:S(2)}) copy-start(pred[8,2,8,16]{3,2,1,0:T(8,128)(4,1)} %copy-done.11) | copy-start | bytes 6148
  90.6 5.6 %copy-start.23 = (f32[16,8]{1,0:T(8,128)S(1)}, f32[16,8]{1,0:T(8,128)}, u32[]{:S(2)}) copy-start(f32[16,8]{1,0:T(8,128)} %get-tuple-element.44) | copy-start | bytes 1540
  90.6 5.7 %copy-start.22 = (f32[16,8]{1,0:T(8,128)S(1)}, f32[16,8]{1,0:T(8,128)}, u32[]{:S(2)}) copy-start(f32[16,8]{1,0:T(8,128)} %get-tuple-element.72) | copy-start | bytes 1540
  95.5 5.4 %collective-permute-start = (f32[1,16,32]{2,1,0:T(8,128)S(1)}, f32[1,16,32]{2,1,0:T(8,128)S(1)}, u32[]{:S(2)}, u32[]{:S(2)}) collective-permute-start(f32[1,16,32]{2,1,0:T(8,128)S(1)} %get-tuple-element.36), channel_id=1, source_target_pairs={{0,2},{2,0},{4,6},{6,4},{8,10},{10,8},{12,14},{14,12},{1,3},{3,1},... | collective-permute-start | bytes 6152 | tf_op jit(solution)/shard_map/ppermute | solution.py:164
  96.1 48.0 %copy-start.1 = (s32[128,1]{0,1:T(1,128)S(1)}, s32[128,1]{0,1:T(1,128)}, u32[]{:S(2)}) copy-start(s32[128,1]{0,1:T(1,128)} %param.10) | copy-start | bytes 1540
  96.6 27.2 %collective-permute-start.1 = (f32[1,16,32]{2,1,0:T(8,128)S(1)}, f32[1,16,32]{2,1,0:T(8,128)S(1)}, u32[]{:S(2)}, u32[]{:S(2)}) collective-permute-start(f32[1,16,32]{2,1,0:T(8,128)S(1)} %get-tuple-element.35), channel_id=1, source_target_pairs={{0,4},{2,6},{4,0},{6,2},{8,12},{10,14},{12,8},{14,10},{1,5},{3,7},... | collective-permute-start | bytes 6152 | tf_op jit(solution)/shard_map/ppermute | solution.py:164
  98.2 28.0 %collective-permute-start.2 = (f32[1,16,32]{2,1,0:T(8,128)S(1)}, f32[1,16,32]{2,1,0:T(8,128)S(1)}, u32[]{:S(2)}, u32[]{:S(2)}) collective-permute-start(f32[1,16,32]{2,1,0:T(8,128)S(1)} %get-tuple-element.34), channel_id=1, source_target_pairs={{0,6},{2,4},{4,2},{6,0},{8,14},{10,12},{12,10},{14,8},{1,7},{3,5},... | collective-permute-start | bytes 6152 | tf_op jit(solution)/shard_map/ppermute | solution.py:164
  98.2 40.5 %collective-permute-start.3 = (f32[1,16,32]{2,1,0:T(8,128)S(1)}, f32[1,16,32]{2,1,0:T(8,128)S(1)}, u32[]{:S(2)}, u32[]{:S(2)}) collective-permute-start(f32[1,16,32]{2,1,0:T(8,128)S(1)} %get-tuple-element.33), channel_id=1, source_target_pairs={{0,8},{2,10},{4,12},{6,14},{8,0},{10,2},{12,4},{14,6},{1,9},{3,11}... | collective-permute-start | bytes 6152 | tf_op jit(solution)/shard_map/ppermute | solution.py:164
  100.8 37.9 %collective-permute-start.4 = (f32[1,16,32]{2,1,0:T(8,128)S(1)}, f32[1,16,32]{2,1,0:T(8,128)S(1)}, u32[]{:S(2)}, u32[]{:S(2)}) collective-permute-start(f32[1,16,32]{2,1,0:T(8,128)S(1)} %get-tuple-element.32), channel_id=1, source_target_pairs={{0,10},{2,8},{4,14},{6,12},{8,2},{10,0},{12,6},{14,4},{1,11},{3,9}... | collective-permute-start | bytes 6152 | tf_op jit(solution)/shard_map/ppermute | solution.py:164
  101.0 37.8 %collective-permute-start.5 = (f32[1,16,32]{2,1,0:T(8,128)S(1)}, f32[1,16,32]{2,1,0:T(8,128)S(1)}, u32[]{:S(2)}, u32[]{:S(2)}) collective-permute-start(f32[1,16,32]{2,1,0:T(8,128)S(1)} %get-tuple-element.31), channel_id=1, source_target_pairs={{0,12},{2,14},{4,8},{6,10},{8,4},{10,6},{12,0},{14,2},{1,13},{3,15... | collective-permute-start | bytes 6152 | tf_op jit(solution)/shard_map/ppermute | solution.py:164
  123.8 15.0 %collective-permute-start.6 = (f32[1,16,32]{2,1,0:T(8,128)S(1)}, f32[1,16,32]{2,1,0:T(8,128)S(1)}, u32[]{:S(2)}, u32[]{:S(2)}) collective-permute-start(f32[1,16,32]{2,1,0:T(8,128)S(1)} %get-tuple-element.30), channel_id=1, source_target_pairs={{0,14},{2,12},{4,10},{6,8},{8,6},{10,4},{12,2},{14,0},{1,15},{3,13... | collective-permute-start | bytes 6152 | tf_op jit(solution)/shard_map/ppermute | solution.py:164
